TPU v7x, 32 devices: a whole 2x2x4 slice. The times are simulated.
32 devices in a mesh: dp: 4 (over y, x), fsdp: 8 (over z, core).
Axes of the slice: x: 2, y: 2, z: 4, core: 2. Of those that a mesh axis runs over, the one named last changes fastest.
Arguments:
- tokens: bfloat16 [32768, 768], P(('dp', 'fsdp')), may hold values from -11 to 11
- attention: bfloat16 [768, 3072], P(None, 'fsdp'), may hold values from -2 to 2
- attvector: bfloat16 [3840], P('fsdp'), may hold values from -2 to 2
- expand: bfloat16 [768, 3072], P(None, 'fsdp'), may hold values from -0.21875 to 0.21875
- contract: bfloat16 [3072, 768], P('fsdp'), may hold values from -0.109375 to 0.109375
- feedvector: bfloat16 [5376], P('fsdp'), may hold values from -2 to 2
- lengths: int32 [64], P(('dp', 'fsdp')), may hold values from 1 to 512, 19660 in all
- cotangent: bfloat16 [32768, 768], P(('dp', 'fsdp')), may hold values from -6 to 6
Outputs:
- layer_output: bfloat16 [32768, 768], P(('dp', 'fsdp'))
- input_grad: bfloat16 [32768, 768], P(('dp', 'fsdp'))
- attention_grad: float32 [768, 3072], P(None, 'fsdp')
- attvector_grad: float32 [3840], P('fsdp')
- expand_grad: float32 [768, 3072], P(None, 'fsdp')
- contract_grad: float32 [3072, 768], P('fsdp')
- feedvector_grad: float32 [5376], P('fsdp')
- root_squares: float32 [3], replicated
Inputs may be any that keep to these rules, and one draw needn't show every extreme that they name: `lengths`: some row is full.
All inputs are finite; a program needn't handle non-finite values. No bound on the sum of `lengths` on one device may be relied on, other than what follows from the above.
Results may differ from a plain program's by a relative error of at most 0.015.
Values may be sent and summed in bfloat16 or wider, within the bound.
No kernel may reach another device: no remote copies, remote signals or barrier semaphores. Data moves between devices by JAX's collectives and lax.ppermute only.
A program may use at most 192 MiB of HBM per device.

v0:
```python
import math
import jax
import jax.numpy as jnp
from jax import lax
from jax.sharding import PartitionSpec as P

HEAD_DIM = 64
FF = 3072
EPSILON = 1e-12
NEGATIVE = -1000000000.0


def norm_forward(residual, scale_gain, shift_bias):
    centered = residual - jnp.mean(residual, axis=-1, keepdims=True)
    inverse = lax.rsqrt(jnp.mean(centered * centered, axis=-1, keepdims=True) + EPSILON)
    normed = centered * inverse
    return (normed * scale_gain + shift_bias, normed, inverse)


def norm_backward(upstream, normed, inverse, scale_gain):
    gain_grad = jnp.sum(upstream * normed, axis=0)
    shift_grad = jnp.sum(upstream, axis=0)
    scaled = upstream * scale_gain
    mean_plain = jnp.mean(scaled, axis=-1, keepdims=True)
    mean_normed = jnp.mean(scaled * normed, axis=-1, keepdims=True)
    return (inverse * (scaled - mean_plain - normed * mean_normed), gain_grad, shift_grad)


def masked_scores(queries, key_rows, live_mask):
    scale_factor = 1.0 / math.sqrt(queries.shape[-1])
    scores = (
        jnp.einsum("qhd,khd->hqk", queries, key_rows, preferred_element_type=jnp.float32)
        * scale_factor
    )
    return jnp.where(live_mask[None, None, :], scores, NEGATIVE)


def attend(block_item):
    queries, key_rows, value_rows, live_mask = block_item
    scores = masked_scores(queries, key_rows, live_mask)
    peak_score = jnp.max(scores, axis=-1, keepdims=True)
    totals = jnp.sum(jnp.exp(scores - peak_score), axis=-1, keepdims=True)
    logsum = peak_score + jnp.log(totals)
    softmax_low = jnp.exp(scores - logsum).astype(jnp.bfloat16)
    context = jnp.einsum(
        "hqk,khd->qhd", softmax_low, value_rows, preferred_element_type=jnp.float32
    )
    return (context.astype(jnp.bfloat16), logsum[..., 0])


def attend_back(block_item):
    queries, key_rows, value_rows, live_mask, logsum, context_grad = block_item
    scale_factor = 1.0 / math.sqrt(queries.shape[-1])
    scores = masked_scores(queries, key_rows, live_mask)
    softmax_wide = jnp.exp(scores - logsum[..., None])
    softmax_low = softmax_wide.astype(jnp.bfloat16)
    value_grad = jnp.einsum(
        "hqk,qhd->khd", softmax_low, context_grad, preferred_element_type=jnp.float32
    )
    weight_grad = jnp.einsum(
        "qhd,khd->hqk", context_grad, value_rows, preferred_element_type=jnp.float32
    )
    row_total = jnp.sum(softmax_wide * weight_grad, axis=-1, keepdims=True)
    score_grad = (softmax_wide * (weight_grad - row_total)).astype(jnp.bfloat16)
    query_grad = (
        jnp.einsum("hqk,khd->qhd", score_grad, key_rows, preferred_element_type=jnp.float32)
        * scale_factor
    )
    key_grad = (
        jnp.einsum("hqk,qhd->khd", score_grad, queries, preferred_element_type=jnp.float32)
        * scale_factor
    )
    return (
        query_grad.astype(jnp.bfloat16),
        key_grad.astype(jnp.bfloat16),
        value_grad.astype(jnp.bfloat16),
    )


def gelu_slope(inner_act):
    cumulative = 0.5 * (1.0 + lax.erf(inner_act * (1.0 / math.sqrt(2.0))))
    density = jnp.exp(-0.5 * inner_act * inner_act) * (1.0 / math.sqrt(2.0 * math.pi))
    return cumulative + inner_act * density


def column_sum(values):
    return jnp.sum(values, axis=0, dtype=jnp.float32)


def per_device(tokens, attention, attvector, expand, contract, feedvector, lengths, cotangent):
    model_width = tokens.shape[1]
    row_count = lengths.shape[0]
    positions = tokens.shape[0] // row_count
    head_count = model_width // HEAD_DIM
    attn_whole, attvec_whole = (
        lax.all_gather(attention, "fsdp", axis=1, tiled=True),
        lax.all_gather(attvector, "fsdp", axis=0, tiled=True),
    )
    expand_whole, contract_whole, feedvec_whole = (
        lax.all_gather(expand, "fsdp", axis=1, tiled=True),
        lax.all_gather(contract, "fsdp", axis=0, tiled=True),
        lax.all_gather(feedvector, "fsdp", axis=0, tiled=True),
    )
    attvec_wide = attvec_whole.astype(jnp.float32)
    feedvec_wide = feedvec_whole.astype(jnp.float32)
    query_bias = attvec_wide[:model_width]
    value_bias = attvec_wide[model_width : 2 * model_width]
    output_bias = attvec_wide[2 * model_width : 3 * model_width]
    first_gain = attvec_wide[3 * model_width : 4 * model_width]
    first_shift = attvec_wide[4 * model_width :]
    inner_bias = feedvec_wide[:FF]
    outer_bias = feedvec_wide[FF : FF + model_width]
    second_gain = feedvec_wide[FF + model_width : FF + 2 * model_width]
    second_shift = feedvec_wide[FF + 2 * model_width :]
    tokens_wide = tokens.astype(jnp.float32)
    projected = jnp.dot(
        tokens, attn_whole[:, : 3 * model_width], preferred_element_type=jnp.float32
    )
    queries = (projected[:, :model_width] + query_bias).astype(jnp.bfloat16)
    key_rows = projected[:, model_width : 2 * model_width].astype(jnp.bfloat16)
    value_rows = (projected[:, 2 * model_width :] + value_bias).astype(jnp.bfloat16)
    shape_four = (row_count, positions, head_count, HEAD_DIM)
    live_mask = jnp.arange(positions, dtype=jnp.int32)[None, :] < lengths[:, None]
    query_four = queries.reshape(shape_four)
    key_four = key_rows.reshape(shape_four)
    value_four = value_rows.reshape(shape_four)
    context, logsum = lax.map(attend, (query_four, key_four, value_four, live_mask))
    context_flat = context.reshape(-1, model_width)
    branch_attn = (
        jnp.dot(context_flat, attn_whole[:, 3 * model_width :], preferred_element_type=jnp.float32)
        + output_bias
    )
    hidden, normed_one, inverse_one = norm_forward(
        tokens_wide + branch_attn, first_gain, first_shift
    )
    hidden_low = hidden.astype(jnp.bfloat16)
    inner_act = jnp.dot(hidden_low, expand_whole, preferred_element_type=jnp.float32) + inner_bias
    gelu_low = jax.nn.gelu(inner_act, approximate=False).astype(jnp.bfloat16)
    branch_feed = jnp.dot(gelu_low, contract_whole, preferred_element_type=jnp.float32) + outer_bias
    result, normed_two, inverse_two = norm_forward(hidden + branch_feed, second_gain, second_shift)
    live_column = live_mask.reshape(-1, 1).astype(jnp.float32)
    squares = jnp.stack(
        [
            jnp.sum(live_column * tokens_wide * tokens_wide),
            jnp.sum(live_column * branch_attn * branch_attn),
            jnp.sum(live_column * branch_feed * branch_feed),
        ]
    )
    count_sum = jnp.sum(lengths).astype(jnp.float32)
    square_sums, count_total = lax.psum((squares, count_sum), ("dp", "fsdp"))
    root_squares = jnp.sqrt(square_sums / (count_total * model_width))
    back_attention, back_attvec = (
        lax.all_gather(attention, "fsdp", axis=1, tiled=True),
        lax.all_gather(attvector, "fsdp", axis=0, tiled=True),
    )
    back_expand, back_contract, back_feedvec = (
        lax.all_gather(expand, "fsdp", axis=1, tiled=True),
        lax.all_gather(contract, "fsdp", axis=0, tiled=True),
        lax.all_gather(feedvector, "fsdp", axis=0, tiled=True),
    )
    first_gain_back = back_attvec[3 * model_width : 4 * model_width].astype(jnp.float32)
    second_gain_back = back_feedvec[FF + model_width : FF + 2 * model_width].astype(jnp.float32)
    grad_two, second_gain_grad, second_shift_grad = norm_backward(
        cotangent.astype(jnp.float32), normed_two, inverse_two, second_gain_back
    )
    feed_out_grad = grad_two.astype(jnp.bfloat16)
    outer_bias_grad = column_sum(feed_out_grad)
    contract_grad = jnp.einsum(
        "nf,nd->fd", gelu_low, feed_out_grad, preferred_element_type=jnp.float32
    )
    gelu_grad = jnp.einsum(
        "nd,fd->nf", feed_out_grad, back_contract, preferred_element_type=jnp.float32
    )
    inner_grad = (gelu_grad * gelu_slope(inner_act)).astype(jnp.bfloat16)
    inner_bias_grad = column_sum(inner_grad)
    expand_grad = jnp.einsum(
        "nd,nf->df", hidden_low, inner_grad, preferred_element_type=jnp.float32
    )
    feedvec_grad = jnp.concatenate(
        [inner_bias_grad, outer_bias_grad, second_gain_grad, second_shift_grad]
    )
    feed_shards = (
        lax.psum_scatter(expand_grad, "fsdp", scatter_dimension=1, tiled=True),
        lax.psum_scatter(contract_grad, "fsdp", scatter_dimension=0, tiled=True),
        lax.psum_scatter(feedvec_grad, "fsdp", scatter_dimension=0, tiled=True),
    )
    hidden_grad = grad_two + jnp.einsum(
        "nf,df->nd", inner_grad, back_expand, preferred_element_type=jnp.float32
    )
    grad_one, first_gain_grad, first_shift_grad = norm_backward(
        hidden_grad, normed_one, inverse_one, first_gain_back
    )
    attn_out_grad = grad_one.astype(jnp.bfloat16)
    output_bias_grad = column_sum(attn_out_grad)
    output_weight_grad = jnp.einsum(
        "nd,ne->de", context_flat, attn_out_grad, preferred_element_type=jnp.float32
    )
    context_grad = jnp.einsum(
        "ne,de->nd",
        attn_out_grad,
        back_attention[:, 3 * model_width :],
        preferred_element_type=jnp.float32,
    ).astype(jnp.bfloat16)
    query_grad, key_grad, value_grad = lax.map(
        attend_back,
        (query_four, key_four, value_four, live_mask, logsum, context_grad.reshape(shape_four)),
    )
    projected_grad = jnp.concatenate(
        [
            query_grad.reshape(-1, model_width),
            key_grad.reshape(-1, model_width),
            value_grad.reshape(-1, model_width),
        ],
        axis=1,
    )
    query_bias_grad = column_sum(projected_grad[:, :model_width])
    value_bias_grad = column_sum(projected_grad[:, 2 * model_width :])
    projection_grad = jnp.einsum(
        "nd,ne->de", tokens, projected_grad, preferred_element_type=jnp.float32
    )
    input_grad = grad_one + jnp.einsum(
        "ne,de->nd",
        projected_grad,
        back_attention[:, : 3 * model_width],
        preferred_element_type=jnp.float32,
    )
    attention_grad = jnp.concatenate([projection_grad, output_weight_grad], axis=1)
    attvec_grad = jnp.concatenate(
        [query_bias_grad, value_bias_grad, output_bias_grad, first_gain_grad, first_shift_grad]
    )
    attn_shards = (
        lax.psum_scatter(attention_grad, "fsdp", scatter_dimension=1, tiled=True),
        lax.psum_scatter(attvec_grad, "fsdp", scatter_dimension=0, tiled=True),
    )
    finished = (
        lax.psum(attn_shards[0].astype(jnp.bfloat16), "dp").astype(jnp.float32),
        lax.psum(attn_shards[1].astype(jnp.bfloat16), "dp").astype(jnp.float32),
        lax.psum(feed_shards[0].astype(jnp.bfloat16), "dp").astype(jnp.float32),
        lax.psum(feed_shards[1].astype(jnp.bfloat16), "dp").astype(jnp.float32),
        lax.psum(feed_shards[2].astype(jnp.bfloat16), "dp").astype(jnp.float32),
    )
    return (
        result.astype(jnp.bfloat16),
        input_grad.astype(jnp.bfloat16),
        finished[0],
        finished[1],
        finished[2],
        finished[3],
        finished[4],
        root_squares,
    )


def solution(mesh):
    return jax.shard_map(
        per_device,
        mesh=mesh,
        in_specs=(
            P(("dp", "fsdp"), None),
            P(None, "fsdp"),
            P("fsdp"),
            P(None, "fsdp"),
            P("fsdp", None),
            P("fsdp"),
            P(("dp", "fsdp")),
            P(("dp", "fsdp"), None),
        ),
        out_specs=(
            P(("dp", "fsdp"), None),
            P(("dp", "fsdp"), None),
            P(None, "fsdp"),
            P("fsdp"),
            P(None, "fsdp"),
            P("fsdp", None),
            P("fsdp"),
            P(),
        ),
        check_vma=False,
    )
```

profile of v0, /device:TPU:0, one launch (start us, length us, event | category | flops | bytes accessed | tf_op | source)
XLA Modules:
  0.0 590.4 jit_solution(3069860904495769675)
XLA Ops:
  13.8 32.2 %all-reduce.6 = (bf16[3840]{0:T(1024)(128)(2,1)S(1)}, bf16[5376]{0:T(1024)(128)(2,1)S(1)}) all-reduce(bf16[3840]{0:T(1024)(128)(2,1)S(1)} %dynamic-update-slice, bf16[5376]{0:T(1024)(128)(2,1)S(1)} %dynamic-update-slice.1), channel_id=1, replica_groups=mesh['dp'=4,'fsdp'=8] {'fsdp'}, use_global_device_ids=true, to_apply=%add | all-reduce | flops 9216 | bytes 36864
  48.6 2.6 copy.75
  52.8 11.5 %all-gather.4.cloned.1.call-done = bf16[768,3072]{1,0:T(8,128)(2,1)} async-done(((bf16[768,384]{1,0:T(8,128)(2,1)}), bf16[768,3072]{1,0:T(8,128)(2,1)}) %all-gather.4.cloned.1.call-update) | async-done | bytes 4718608 | tf_op jit(solution)/shard_map/all_gather | solution.py:96
  64.3 5.8 fusion.87
  70.3 2.3 fusion.83
  74.6 2.4 reshape.146
  80.3 3.9 reshape.147
  85.9 2.6 copy.67
  88.5 3.9 reshape.145
  92.4 2.9 copy.70
  96.6 19.2 %while.26 = (s32[]{:T(128)}, bf16[2,512,12,64]{1,3,2,0:T(8,128)(2,1)}, f32[2,12,512]{2,1,0:T(8,128)S(1)}, bf16[2,512,12,64]{1,3,2,0:T(8,128)(2,1)}, pred[2,512]{...) while((s32[]{:T(128)}, ...), condition=%wide.region_3.4_spmd, body=%wide.region_0.3_spmd.sunk | while | flops 840296448 | bytes 47428224 | solution.py:127
  96.8 3.1 fusion.144
  99.9 2.6 exponential_reduce_fusion.2
  102.5 3.8 fusion.145
  106.3 3.1 fusion.144
  109.4 2.6 exponential_reduce_fusion.2
  112.1 3.7 fusion.145
  115.8 4.2 copy.73
  120.5 5.1 fusion.105
  126.1 38.3 %fusion.59 = (bf16[1024,3072]{1,0:T(8,128)(2,1)}, f32[1024,3072]{1,0:T(8,128)}) fusion(f32[3072]{0:T(1024)S(1)} %slice.77, bf16[768,3072]{1,0:T(8,128)(2,1)} %all-gather.6.cloned.1.call-done, f32[1024,768]{0,1:T(8,128)S(1)} %get-tuple-element.245, f32[768]{0:T(1024)S(1)} %get-tuple-element.259, f32[768]{0:T(1024)S(1)} %get-tuple-element.258, ...), kind=kOutput, calls=%fused_computation.67 | convolution fusion | flops 5043388416 | bytes 26765312 | tf_op jit(solution)/shard_map/dot_general | solution.py:137
  164.4 3.2 all-gather.8.cloned.1.call-done
  167.6 12.3 %fusion.80 = (f32[]{:T(128)}, f32[]{:T(128)}, f32[]{:T(128)}, f32[1024]{0:T(1024)S(1)}, f32[1024,768]{0,1:T(8,128)S(1)}) fusion(bf16[1024,768]{0,1:T(8,128)(2,1)} %copy.66, f32[1024]{0:T(1024)S(1)} %bitcast.165, f32[1024,768]{0,1:T(8,128)} %get-tuple-element.267, f32[768]{0:T(1024)S(1)} %get-tuple-element.260, f32[768]{0:T(1024)S(1)} %copy-done.46, ...), kind=kOutput, calls=%fused_computation.106 | convolution fusion | flops 4845992960 | bytes 22048780 | tf_op jit(solution)/shard_map/dot_general | solution.py:139
  183.2 3.3 convert_reduce_fusion.2
  186.5 12.3 %convert_reduce_fusion = (f32[3072]{0:T(1024)}, bf16[1024,3072]{1,0:T(8,128)(2,1)S(1)}) fusion(f32[1024,3072]{1,0:T(8,128)S(1)} %copy-done.49, f32[3072]{0:T(1024)S(1)} %slice.77, bf16[1024,768]{0,1:T(8,128)(2,1)S(1)} %get-tuple-element.239, bf16[3072,768]{1,0:T(8,128)(2,1)S(1)} %bitcast.167), kind=kOutput, calls=%fused_computation.74 | convolution fusion | flops 4872729600 | bytes 25190400 | tf_op jit(solution)/shard_map/nd,fd->nf/dot_general | solution.py:171
  198.8 2.6 copy-done.48
  201.4 7.8 %fusion.99 = f32[768,3072]{1,0:T(8,128)} fusion(bf16[1024,3072]{1,0:T(8,128)(2,1)S(1)} %get-tuple-element.272, f32[1024,768]{0,1:T(8,128)S(1)} %copy-done.15, f32[768]{0:T(1024)S(1)} %get-tuple-element.259, f32[768]{0:T(1024)S(1)} %get-tuple-element.258, f32[1024]{0:T(1024)S(1)} %add_rsqrt_fusion.1, f32[1024]{0:T(1024)S(1)} %broadcast_multiply_fusion.5), kind=kOutput, calls=%fused_computation.169 | convolution fusion | flops 4835770368 | bytes 18888704 | tf_op jit(solution)/shard_map/nd,nf->df/dot_general | solution.py:176
  209.9 12.5 %multiply_reduce_fusion.1 = (f32[768]{0:T(1024)}, f32[1024]{0:T(1024)S(1)}, f32[1024]{0:T(1024)S(1)}, f32[768]{0:T(1024)}, f32[1024,768]{0,1:T(8,128)S(1)}) fusion(f32[1024,768]{0,1:T(8,128)} %copy-done.14, f32[1024]{0:T(1024)S(1)} %add_rsqrt_fusion.1, f32[1024]{0:T(1024)S(1)} %broadcast_multiply_fusion.5, f32[768]{0:T(1024)S(1)} %copy-done.36, ...), kind=kOutput, calls=%fused_computation.115 | convolution fusion | flops 4845989888 | bytes 22065152 | tf_op jit(solution)/shard_map/nf,df->nd/dot_general | solution.py:187
  225.7 2.7 convolution_convert_fusion
  235.9 48.7 %while.27 = (s32[]{:T(128)}, bf16[2,512,12,64]{1,3,2,0:T(8,128)(2,1)}, bf16[2,512,12,64]{1,3,2,0:T(8,128)(2,1)}, bf16[2,512,12,64]{1,3,2,0:T(8,128)(2,1)}, bf16[...) while((s32[]{:T(128)}, ...), condition=%wide.region_14.15_spmd, body=%wide.region_12.14_spmd.sunk | while | flops 2062411776 | bytes 152764272 | solution.py:204
  238.1 3.1 fusion.157
  241.2 7.4 %multiply_reduce_fusion.7 = (f32[12,512]{1,0:T(8,128)S(1)}, f32[12,512,512]{1,2,0:T(8,128)}) fusion(f32[12,512,512]{1,2,0:T(8,128)S(1)} %fusion.154, f32[12,512]{1,0:T(8,128)S(1)} %dynamic-slice_bitcast_fusion.2, pred[512]{0:T(512)(128)(4,1)S(1)} %dynamic-slice_reduce_fusion.5, bf16[2,512,12,64]{1,3,2,0:T(8,128)(2,1)S(1)} %copy-done.5, ...), kind=kOutput, calls=%fused_computation.24.clone.1 | convolution fusion | flops 418375680 | bytes 26797568 | tf_op jit(solution)/shard_map/while/body/eval_jaxpr/qhd,khd->hqk/dot_general | solution.py:60
  248.5 7.3 %multiply_convert_fusion.4 = bf16[12,512,512]{1,2,0:T(8,128)(2,1)S(1)} fusion(f32[12,512,512]{1,2,0:T(8,128)} %get-tuple-element.389, f32[12,512,512]{1,2,0:T(8,128)S(1)} %fusion.154, f32[12,512]{1,0:T(8,128)S(1)} %get-tuple-element.390, f32[12,512]{1,0:T(8,128)S(1)} %dynamic-slice_bitcast_fusion.2, pred[512]{0:T(512)(128)(4,1)S(1)} %dynamic-slice_reduce_fusion.5), kind=kLoop, calls=%fused_computation.23.clone.1 | loop fusion | flops 18874368 | bytes 31506944 | tf_op jit(solution)/shard_map/while/body/eval_jaxpr/convert_element_type | solution.py:64
  262.2 3.1 fusion.157
  265.3 7.4 %multiply_reduce_fusion.7 = (f32[12,512]{1,0:T(8,128)S(1)}, f32[12,512,512]{1,2,0:T(8,128)}) fusion(f32[12,512,512]{1,2,0:T(8,128)S(1)} %fusion.154, f32[12,512]{1,0:T(8,128)S(1)} %dynamic-slice_bitcast_fusion.2, pred[512]{0:T(512)(128)(4,1)S(1)} %dynamic-slice_reduce_fusion.5, bf16[2,512,12,64]{1,3,2,0:T(8,128)(2,1)S(1)} %copy-done.5, ...), kind=kOutput, calls=%fused_computation.24.clone.1 | convolution fusion | flops 418375680 | bytes 26797568 | tf_op jit(solution)/shard_map/while/body/eval_jaxpr/qhd,khd->hqk/dot_general | solution.py:60
  272.6 7.2 %multiply_convert_fusion.4 = bf16[12,512,512]{1,2,0:T(8,128)(2,1)S(1)} fusion(f32[12,512,512]{1,2,0:T(8,128)} %get-tuple-element.389, f32[12,512,512]{1,2,0:T(8,128)S(1)} %fusion.154, f32[12,512]{1,0:T(8,128)S(1)} %get-tuple-element.390, f32[12,512]{1,0:T(8,128)S(1)} %dynamic-slice_bitcast_fusion.2, pred[512]{0:T(512)(128)(4,1)S(1)} %dynamic-slice_reduce_fusion.5), kind=kLoop, calls=%fused_computation.23.clone.1 | loop fusion | flops 18874368 | bytes 31506944 | tf_op jit(solution)/shard_map/while/body/eval_jaxpr/convert_element_type | solution.py:64
  284.6 3.2 copy.83
  294.9 2.9 fusion.96
  297.8 5.8 convolution_bitcast_fusion
  303.6 8.0 %pad_maximum_fusion = f32[768,3072]{0,1:T(8,128)} fusion(f32[768,768]{0,1:T(8,128)} %fusion.96, f32[768,2304]{0,1:T(8,128)} %convolution_bitcast_fusion), kind=kLoop, calls=%fused_computation.90 | loop fusion | flops 2359296 | bytes 18874368 | tf_op jit(solution)/shard_map/concatenate | solution.py:227
  311.7 10.0 %fusion.109 = f32[3072,768]{1,0:T(8,128)} fusion(bf16[1024,3072]{1,0:T(8,128)(2,1)} %get-tuple-element.268, bf16[1024,768]{0,1:T(8,128)(2,1)} %copy-done.27), kind=kOutput, calls=%fused_computation.176 | convolution fusion | flops 4831838208 | bytes 17301504 | tf_op jit(solution)/shard_map/nf,nd->fd/dot_general | solution.py:168
  326.9 40.2 %all-reduce.4 = (f32[3]{0:T(128)S(1)}, f32[]{:T(128)}) all-reduce(f32[3]{0:T(128)S(1)} %pad_maximum_fusion.2, f32[]{:T(128)S(6)} %convert_element_type.176), channel_id=1, replica_groups=mesh['dp'=4,'fsdp'=8] {'dp','fsdp'}, use_global_device_ids=true, to_apply=%region_37.38 | all-reduce | flops 4 | bytes 32 | tf_op jit(solution)/shard_map/psum | solution.py:150
  370.1 40.7 %reduce-scatter.4.cloned.1.call-done = f32[768,384]{0,1:T(8,128)} async-done(((f32[768,3072]{0,1:T(8,128)}), f32[768,384]{0,1:T(8,128)}) %reduce-scatter.4.cloned.1.call-update) | async-done | bytes 1179664 | tf_op jit(solution)/shard_map/reduce_scatter | solution.py:232
  412.9 97.9 %reduce-scatter.8.cloned.1.call-done = f32[384,768]{1,0:T(8,128)} async-done(((f32[3072,768]{1,0:T(8,128)}), f32[384,768]{1,0:T(8,128)}) %reduce-scatter.8.cloned.1.call-update) | async-done | bytes 1179664 | tf_op jit(solution)/shard_map/reduce_scatter | solution.py:184
  513.2 26.4 %all-reduce.5 = (bf16[3840]{0:T(1024)(128)(2,1)S(1)}, bf16[5376]{0:T(1024)(128)(2,1)S(1)}) all-reduce(f32[3840]{0:T(1024)S(1)} %constant_dynamic-update-slice_fusion.6, f32[5376]{0:T(1024)S(1)} %pad_maximum_fusion.1), channel_id=3, replica_groups=mesh['dp'=4,'fsdp'=8] {'fsdp'}, use_global_device_ids=true, to_apply=%region_22.23.clone | all-reduce | flops 9216 | bytes 55296
  539.7 9.9 %all-reduce.7 = (bf16[480]{0:T(512)(128)(2,1)S(1)}, bf16[672]{0:T(1024)(128)(2,1)S(1)}) all-reduce(bf16[480]{0:T(512)(128)(2,1)S(1)} %dynamic-slice.9, bf16[672]{0:T(1024)(128)(2,1)S(1)} %dynamic-slice.8), channel_id=1, replica_groups=mesh['dp'=4,'fsdp'=8] {'dp'}, use_global_device_ids=true, to_apply=%region_23.24 | all-reduce | flops 1152 | bytes 4608 | tf_op jit(solution)/shard_map/psum | solution.py:237
  552.4 8.3 %add_convert_fusion = bf16[1024,768]{0,1:T(8,128)(2,1)S(1)} fusion(f32[1024,768]{0,1:T(8,128)} %copy-done.20, bf16[1024,2304]{0,1:T(8,128)(2,1)} %copy-done.29, bf16[768,3072]{1,0:T(8,128)(2,1)} %all-gather.4.cloned.1.call-done), kind=kOutput, calls=%fused_computation.119 | convolution fusion | flops 3625451520 | bytes 12976128 | tf_op jit(solution)/shard_map/ne,de->nd/dot_general | solution.py:221
  563.4 14.3 %all-reduce.11.cloned.1.call-done = (bf16[768,384]{0,1:T(8,128)(2,1)}, bf16[768,384]{1,0:T(8,128)(2,1)}, bf16[384,768]{1,0:T(8,128)(2,1)}) async-done(((bf16[768,384]{0,1:T(8,128)(2,1)}, bf16[768,384]{1,0:T(8,128)(2,1)}, bf16[384,768]{1,0:T(8,128)(2,1)}), (bf16[768,384]{0,1:T(8,128)(2,1)}, bf16[768,384]{1,0:T(8,128)(2,1)}, bf16[384,768]{1,0:T(8,128)(2,1)})) %all-reduce.11.cloned.1.call-update) | async-done | bytes 1769488 | tf_op jit(solution)/shard_map/psum | solution.py:236
  577.7 2.4 copy.88
  (223 shorter events, 71.9 us)
Async XLA Ops:
  7.2 44.0 %copy-start.22 = (bf16[1024,768]{1,0:T(8,128)(2,1)S(1)}, bf16[1024,768]{1,0:T(8,128)(2,1)}, u32[]{:S(2)}) copy-start(bf16[1024,768]{1,0:T(8,128)(2,1)} %param.12) | copy-start | bytes 4718596
  7.2 57.1 %all-gather.4.cloned.1.call-start = ((), (), s32[]{:S(2)}) async-start(), calls=%async_computation.3 | async-start | bytes 5308416 | tf_op jit(solution)/shard_map/all_gather | solution.py:96
  7.9 118.2 %all-gather.6.cloned.1.call-start = ((), (), s32[]{:S(2)}) async-start(), calls=%async_computation.4 | async-start | bytes 5308416 | tf_op jit(solution)/shard_map/all_gather | solution.py:100
  8.7 158.9 %all-gather.8.cloned.1.call-start = ((), (), s32[]{:S(2)}) async-start(), calls=%async_computation.5 | async-start | bytes 5308416 | tf_op jit(solution)/shard_map/all_gather | solution.py:101
  9.4 358.5 %reduce-scatter.6.cloned.1.call-start = ((), (), s32[]{:S(2)}) async-start(), calls=%async_computation.7 | async-start | bytes 10616832 | tf_op jit(solution)/shard_map/reduce_scatter | solution.py:183
  99.9 2.6 copy-start.4
  115.8 4.7 copy-start
  115.8 4.7 copy-start.2
  115.8 4.7 copy-start.30
  115.8 4.7 copy-start.32
  115.8 4.7 copy-start.26
  120.5 5.1 copy-start.24
  125.6 38.8 %copy-start.14 = (f32[1024,768]{0,1:T(8,128)}, f32[1024,768]{0,1:T(8,128)S(1)}, u32[]{:S(2)}) copy-start(f32[1024,768]{0,1:T(8,128)S(1)} %get-tuple-element.245) | copy-start | bytes 9437188
  126.1 41.5 %copy-start.45 = (f32[1,4,2,128]{3,1,2,0:T(4,128)S(1)}, f32[1,4,2,128]{3,1,2,0:T(4,128)}, u32[]{:S(2)}) copy-start(f32[1,4,2,128]{3,1,2,0:T(4,128)} %copy.100) | copy-start | bytes 12292
  126.1 41.5 %copy-start.46 = (f32[768]{0:T(1024)S(1)}, f32[768]{0:T(1024)}, u32[]{:S(2)}) copy-start(f32[768]{0:T(1024)} %get-tuple-element.257) | copy-start | bytes 9220
  167.6 18.9 %copy-start.49 = (f32[1024,3072]{1,0:T(8,128)S(1)}, f32[1024,3072]{1,0:T(8,128)}, u32[]{:S(2)}) copy-start(f32[1024,3072]{1,0:T(8,128)} %get-tuple-element.269) | copy-start | bytes 37748740
  180.3 2.9 copy-start.38
  180.3 2.9 copy-start.39
  181.3 5.2 slice-start
  183.2 3.3 slice-start.1
  186.5 12.3 %copy-start.27 = (bf16[1024,768]{0,1:T(8,128)(2,1)}, bf16[1024,768]{0,1:T(8,128)(2,1)S(1)}, u32[]{:S(2)}) copy-start(bf16[1024,768]{0,1:T(8,128)(2,1)S(1)} %get-tuple-element.239) | copy-start | bytes 4718596
  186.5 14.9 %copy-start.15 = (f32[1024,768]{0,1:T(8,128)S(1)}, f32[1024,768]{0,1:T(8,128)}, u32[]{:S(2)}) copy-start(f32[1024,768]{0,1:T(8,128)} %copy-done.14) | copy-start | bytes 9437188
  209.2 201.6 %reduce-scatter.4.cloned.1.call-start = ((), (), s32[]{:S(2)}) async-start(), calls=%async_computation.6 | async-start | bytes 10616832 | tf_op jit(solution)/shard_map/reduce_scatter | solution.py:232
  209.9 12.5 %copy-start.16 = (f32[1024,768]{0,1:T(8,128)S(1)}, f32[1024,768]{0,1:T(8,128)}, u32[]{:S(2)}) copy-start(f32[1024,768]{0,1:T(8,128)} %copy-done.14) | copy-start | bytes 9437188
  231.9 4.0 copy-start.1
  231.9 4.0 copy-start.3
  231.9 4.0 copy-start.31
  231.9 4.0 copy-start.33
  238.1 3.1 copy-start.5
  241.2 7.4 %copy-start.8 = (bf16[2,512,12,64]{1,3,2,0:T(8,128)(2,1)}, bf16[2,512,12,64]{1,3,2,0:T(8,128)(2,1)S(1)}, u32[]{:S(2)}) copy-start(bf16[2,512,12,64]{1,3,2,0:T(8,128)(2,1)S(1)} %fusion.157) | copy-start | bytes 4718596 | tf_op jit(solution)/shard_map/while
  248.5 7.4 %copy-start.17 = (bf16[2,512,12,64]{1,3,2,0:T(8,128)(2,1)S(1)}, bf16[2,512,12,64]{1,3,2,0:T(8,128)(2,1)}, u32[]{:S(2)}) copy-start(bf16[2,512,12,64]{1,3,2,0:T(8,128)(2,1)} %get-tuple-element.428) | copy-start | bytes 4718596 | tf_op jit(solution)/shard_map/while
  262.2 3.1 copy-start.5
  265.3 7.4 %copy-start.8 = (bf16[2,512,12,64]{1,3,2,0:T(8,128)(2,1)}, bf16[2,512,12,64]{1,3,2,0:T(8,128)(2,1)S(1)}, u32[]{:S(2)}) copy-start(bf16[2,512,12,64]{1,3,2,0:T(8,128)(2,1)S(1)} %fusion.157) | copy-start | bytes 4718596 | tf_op jit(solution)/shard_map/while
  272.6 7.3 %copy-start.17 = (bf16[2,512,12,64]{1,3,2,0:T(8,128)(2,1)S(1)}, bf16[2,512,12,64]{1,3,2,0:T(8,128)(2,1)}, u32[]{:S(2)}) copy-start(bf16[2,512,12,64]{1,3,2,0:T(8,128)(2,1)} %get-tuple-element.428) | copy-start | bytes 4718596 | tf_op jit(solution)/shard_map/while
  284.6 3.6 copy-start.9
  294.9 2.9 copy-start.29
  294.9 2.9 copy-start.23
  311.6 199.2 %reduce-scatter.8.cloned.1.call-start = ((), (), s32[]{:S(2)}) async-start(), calls=%async_computation.8 | async-start | bytes 10616832 | tf_op jit(solution)/shard_map/reduce_scatter | solution.py:184
  321.7 256.0 %all-reduce.11.cloned.1.call-start = ((), (), s32[]{:S(2)}) async-start(), calls=%async_computation.9 | async-start | bytes 3538944 | tf_op jit(solution)/shard_map/psum | solution.py:236
  367.8 145.2 %copy-start.37 = (f32[768]{0:T(1024)S(1)}, f32[768]{0:T(1024)}, u32[]{:S(2)}) copy-start(f32[768]{0:T(1024)} %get-tuple-element.240) | copy-start | bytes 9220
  367.8 145.3 %copy-start.44 = (f32[768]{0:T(1024)S(1)}, f32[768]{0:T(1024)}, u32[]{:S(2)}) copy-start(f32[768]{0:T(1024)} %get-tuple-element.180) | copy-start | bytes 9220
  367.8 145.3 %copy-start.43 = (f32[768]{0:T(1024)S(1)}, f32[768]{0:T(1024)}, u32[]{:S(2)}) copy-start(f32[768]{0:T(1024)} %get-tuple-element.185) | copy-start | bytes 9220
  367.8 145.3 %copy-start.35 = (f32[768]{0:T(1024)S(1)}, f32[768]{0:T(1024)}, u32[]{:S(2)}) copy-start(f32[768]{0:T(1024)} %get-tuple-element.238) | copy-start | bytes 9220
  367.8 145.3 %copy-start.40 = (f32[768]{0:T(1024)S(1)}, f32[768]{0:T(1024)}, u32[]{:S(2)}) copy-start(f32[768]{0:T(1024)} %get-tuple-element.182) | copy-start | bytes 9220
  367.9 145.3 %copy-start.41 = (f32[768]{0:T(1024)S(1)}, f32[768]{0:T(1024)}, u32[]{:S(2)}) copy-start(f32[768]{0:T(1024)} %get-tuple-element.187) | copy-start | bytes 9220
  367.9 145.3 %copy-start.42 = (f32[3072]{0:T(1024)S(1)}, f32[3072]{0:T(1024)}, u32[]{:S(2)}) copy-start(f32[3072]{0:T(1024)} %get-tuple-element.271) | copy-start | bytes 36868
  370.1 180.8 %copy-start.19 = (bf16[1024,768]{0,1:T(8,128)(2,1)S(1)}, bf16[1024,768]{0,1:T(8,128)(2,1)}, u32[]{:S(2)}) copy-start(bf16[1024,768]{0,1:T(8,128)(2,1)} %get-tuple-element.252) | copy-start | bytes 4718596
  577.7 4.5 copy-start.28
  (20 other events, 33.5 us)
Sparse Core Ops, SparseCore 0:
  9.6 54.6 all-gather.3
  65.9 50.1 all-gather.5
  117.7 49.8 all-gather.7
  209.3 98.1 reduce-scatter.5
  311.8 98.9 reduce-scatter.3
  412.9 97.8 reduce-scatter.7
  514.9 62.7 all-reduce.10
where the time goes:
time: 598 us; the launch traced here: 590 us
  waiting for transfers between devices  170 us (28%)
  matrix products  168 us (28%)
  blocking collectives  109 us (18%)
  local copies, waits for them, and re-layouts  69.8 us (12%)
  other arithmetic  53.7 us (9%)
  between operations  18.8 us (3%)
    reduce_scatter x1, waiting for transfers between devices, per_device(): lax.psum_scatter(contract_grad, 'fsdp', scatter_dimension=0, tiled=True)  97.9 us
    unnamed x2, blocking collectives  58.6 us
    reduce_scatter x1, waiting for transfers between devices, per_device(): lax.psum_scatter(attention_grad, 'fsdp', scatter_dimension=1, tiled=True)  40.7 us
    psum x1, blocking collectives, per_device(): square_sums, count_total = lax.psum((squares, count_sum), ('dp', 'fsdp'))  40.2 us
    dot_general x1, matrix products, per_device(): jnp.dot(hidden_low, expand_whole, preferred_element_type=jnp.float32)  38.3 us
    unnamed x109, local copies, waits for them, and re-layouts  24.2 us
    dot_general x2, matrix products, attend_back(): jnp.einsum('qhd,khd->hqk', context_grad, value_rows, preferred_element_ty...  14.7 us
    convert_element_type x2, other arithmetic, attend_back(): score_grad = (softmax_wide * (weight_grad - row_total)).astype(jnp.bfloat16)  14.6 us
  transfers between devices with their start and end apart: 7, of which 5 were waited for; matrix products, arithmetic and copies ran while one was open for 40% of the time, Pallas kernels for 0%

commit v1 on v0

--- a/solution.py
+++ b/solution.py
@@ -233,7 +233,9 @@
         lax.psum_scatter(attvec_grad, "fsdp", scatter_dimension=0, tiled=True),
     )
     finished = (
-        lax.psum(attn_shards[0].astype(jnp.bfloat16), "dp").astype(jnp.float32),
+        jnp.sum(lax.all_gather(attn_shards[0].astype(jnp.bfloat16), "dp"), axis=0).astype(
+            jnp.float32
+        ),
         lax.psum(attn_shards[1].astype(jnp.bfloat16), "dp").astype(jnp.float32),
         lax.psum(feed_shards[0].astype(jnp.bfloat16), "dp").astype(jnp.float32),
         lax.psum(feed_shards[1].astype(jnp.bfloat16), "dp").astype(jnp.float32),

time: 598 us -> 638 us (1.067)
  waiting for transfers between devices: 170 us -> 194 us
  matrix products: 168 us -> 180 us
    reduce_scatter x1, waiting for transfers between devices: 40.7 us -> 97.8 us  [per_device(): lax.psum_scatter(attention_grad, 'fsdp', scatter_dimension=1, tiled=True)]
    reduce_scatter x1, waiting for transfers between devices: 97.9 us -> 82.7 us  [per_device(): lax.psum_scatter(contract_grad, 'fsdp', scatter_dimension=0, tiled=True)]
    psum x1, waiting for transfers between devices: 14.3 us -> 0.01 us  [per_device(): lax.psum(feed_shards[0].astype(jnp.bfloat16), 'dp').astype(jnp.float32)]
    dot_general x1, matrix products: 38.3 us -> 49.3 us  [per_device(): jnp.dot(hidden_low, expand_whole, preferred_element_type=jnp.float32)]
    unnamed x109 -> x111, local copies, waits for them, and re-layouts: 24.2 us -> 23.7 us
  transfers between devices with their start and end apart: 7 -> 8, of which waited for: 5 -> 3; matrix products, arithmetic and copies ran while one was open for 40% -> 40% of each run, Pallas kernels for 0% -> 0%
where the time goes in v1:
time: 638 us; the launch traced here: 631 us
  waiting for transfers between devices  194 us (30%)
  matrix products  180 us (28%)
  blocking collectives  108 us (17%)
  local copies, waits for them, and re-layouts  71.5 us (11%)
  other arithmetic  57.5 us (9%)
  between operations  19.2 us (3%)
    reduce_scatter x1, waiting for transfers between devices, per_device(): lax.psum_scatter(attention_grad, 'fsdp', scatter_dimension=1, tiled=True)  97.8 us
    reduce_scatter x1, waiting for transfers between devices, per_device(): lax.psum_scatter(contract_grad, 'fsdp', scatter_dimension=0, tiled=True)  82.7 us
    unnamed x2, blocking collectives  60.2 us
    dot_general x1, matrix products, per_device(): jnp.dot(hidden_low, expand_whole, preferred_element_type=jnp.float32)  49.3 us
    psum x1, blocking collectives, per_device(): square_sums, count_total = lax.psum((squares, count_sum), ('dp', 'fsdp'))  38.1 us
    unnamed x111, local copies, waits for them, and re-layouts  23.7 us
    convert_element_type x2, other arithmetic, attend_back(): score_grad = (softmax_wide * (weight_grad - row_total)).astype(jnp.bfloat16)  14.8 us
    dot_general x2, matrix products, attend_back(): jnp.einsum('qhd,khd->hqk', context_grad, value_rows, preferred_element_ty...  14.6 us
  transfers between devices with their start and end apart: 8, of which 3 were waited for; matrix products, arithmetic and copies ran while one was open for 40% of the time, Pallas kernels for 0%

profile of v1, /device:TPU:0, one launch (start us, length us, event | category | flops | bytes accessed | tf_op | source)
XLA Modules:
  0.0 630.5 jit_solution(10529228960058733106)
XLA Ops:
  13.9 32.2 %all-reduce.6 = (bf16[3840]{0:T(1024)(128)(2,1)S(1)}, bf16[5376]{0:T(1024)(128)(2,1)S(1)}) all-reduce(bf16[3840]{0:T(1024)(128)(2,1)S(1)} %dynamic-update-slice, bf16[5376]{0:T(1024)(128)(2,1)S(1)} %dynamic-update-slice.1), channel_id=1, replica_groups=mesh['dp'=4,'fsdp'=8] {'fsdp'}, use_global_device_ids=true, to_apply=%add | all-reduce | flops 9216 | bytes 36864
  48.0 2.7 copy.64
  52.9 11.4 %all-gather.6.cloned.1.call-done = bf16[768,3072]{1,0:T(8,128)(2,1)} async-done(((bf16[768,384]{1,0:T(8,128)(2,1)}), bf16[768,3072]{1,0:T(8,128)(2,1)}) %all-gather.6.cloned.1.call-update) | async-done | bytes 4718608 | tf_op jit(solution)/shard_map/all_gather | solution.py:96
  64.3 5.8 fusion.87
  70.3 2.3 fusion.83
  74.6 2.4 reshape.145
  77.0 2.9 copy.68
  81.6 2.4 reshape.146
  87.3 3.9 reshape.147
  94.2 19.3 %while.26 = (s32[]{:T(128)}, bf16[2,512,12,64]{1,3,2,0:T(8,128)(2,1)}, f32[2,12,512]{2,1,0:T(8,128)S(1)}, bf16[2,512,12,64]{1,3,2,0:T(8,128)(2,1)}, pred[2,512]{...) while((s32[]{:T(128)}, ...), condition=%wide.region_3.4_spmd, body=%wide.region_0.3_spmd.sunk | while | flops 840296448 | bytes 47428216 | solution.py:127
  94.5 3.1 fusion.144
  97.6 2.6 exponential_reduce_fusion.2
  100.2 3.8 fusion.145
  104.0 3.1 fusion.144
  107.1 2.6 exponential_reduce_fusion.2
  109.8 3.7 fusion.145
  113.5 4.2 copy.71
  118.2 5.1 fusion.105
  123.8 49.3 %fusion.59 = (bf16[1024,3072]{1,0:T(8,128)(2,1)}, f32[1024,3072]{1,0:T(8,128)}) fusion(f32[3072]{0:T(1024)S(1)} %slice.77, bf16[768,3072]{1,0:T(8,128)(2,1)} %all-gather.8.cloned.1.call-done, f32[1024,768]{0,1:T(8,128)S(1)} %get-tuple-element.244, f32[768]{0:T(1024)S(1)} %get-tuple-element.258, f32[768]{0:T(1024)S(1)} %get-tuple-element.257, ...), kind=kOutput, calls=%fused_computation.67 | convolution fusion | flops 5043388416 | bytes 26765312 | tf_op jit(solution)/shard_map/dot_general | solution.py:137
  173.2 12.2 %fusion.80 = (f32[]{:T(128)}, f32[]{:T(128)}, f32[]{:T(128)}, f32[1024]{0:T(1024)S(1)}, f32[1024,768]{0,1:T(8,128)S(1)}) fusion(bf16[1024,768]{0,1:T(8,128)(2,1)} %copy.64, f32[1024]{0:T(1024)S(1)} %bitcast.167, f32[1024,768]{0,1:T(8,128)} %get-tuple-element.266, f32[768]{0:T(1024)S(1)} %get-tuple-element.259, f32[768]{0:T(1024)S(1)} %copy-done.45, ...), kind=kOutput, calls=%fused_computation.106 | convolution fusion | flops 4845992960 | bytes 22048780 | tf_op jit(solution)/shard_map/dot_general | solution.py:139
  188.8 3.3 convert_reduce_fusion.2
  192.1 12.3 %convert_reduce_fusion = (f32[3072]{0:T(1024)}, bf16[1024,3072]{1,0:T(8,128)(2,1)S(1)}) fusion(f32[1024,3072]{1,0:T(8,128)S(1)} %copy-done.48, f32[3072]{0:T(1024)S(1)} %slice.77, bf16[1024,768]{0,1:T(8,128)(2,1)S(1)} %get-tuple-element.238, bf16[3072,768]{1,0:T(8,128)(2,1)S(1)} %bitcast.169), kind=kOutput, calls=%fused_computation.74 | convolution fusion | flops 4872729600 | bytes 25190400 | tf_op jit(solution)/shard_map/nd,fd->nf/dot_general | solution.py:171
  204.3 2.6 copy-done.47
  206.9 7.8 %fusion.99 = f32[768,3072]{1,0:T(8,128)} fusion(bf16[1024,3072]{1,0:T(8,128)(2,1)S(1)} %get-tuple-element.271, f32[1024,768]{0,1:T(8,128)S(1)} %copy-done.13, f32[768]{0:T(1024)S(1)} %get-tuple-element.258, f32[768]{0:T(1024)S(1)} %get-tuple-element.257, f32[1024]{0:T(1024)S(1)} %add_rsqrt_fusion.1, f32[1024]{0:T(1024)S(1)} %broadcast_multiply_fusion.5), kind=kOutput, calls=%fused_computation.169 | convolution fusion | flops 4835770368 | bytes 18888704 | tf_op jit(solution)/shard_map/nd,nf->df/dot_general | solution.py:176
  214.8 10.4 %fusion.109 = f32[3072,768]{1,0:T(8,128)} fusion(bf16[1024,3072]{1,0:T(8,128)(2,1)} %get-tuple-element.267, bf16[1024,768]{0,1:T(8,128)(2,1)} %copy-done.27), kind=kOutput, calls=%fused_computation.176 | convolution fusion | flops 4831838208 | bytes 17301504 | tf_op jit(solution)/shard_map/nf,nd->fd/dot_general | solution.py:168
  225.8 12.2 %multiply_reduce_fusion.1 = (f32[768]{0:T(1024)}, f32[1024]{0:T(1024)S(1)}, f32[1024]{0:T(1024)S(1)}, f32[768]{0:T(1024)}, f32[1024,768]{0,1:T(8,128)S(1)}) fusion(f32[1024,768]{0,1:T(8,128)} %copy-done.12, f32[1024]{0:T(1024)S(1)} %add_rsqrt_fusion.1, f32[1024]{0:T(1024)S(1)} %broadcast_multiply_fusion.5, f32[768]{0:T(1024)S(1)} %copy-done.35, ...), kind=kOutput, calls=%fused_computation.115 | convolution fusion | flops 4845989888 | bytes 22065152 | tf_op jit(solution)/shard_map/nf,df->nd/dot_general | solution.py:187
  241.5 2.7 convolution_convert_fusion
  251.7 50.1 %while.27 = (s32[]{:T(128)}, bf16[2,512,12,64]{1,3,2,0:T(8,128)(2,1)}, bf16[2,512,12,64]{1,3,2,0:T(8,128)(2,1)}, bf16[2,512,12,64]{1,3,2,0:T(8,128)(2,1)}, bf16[...) while((s32[]{:T(128)}, ...), condition=%wide.region_14.15_spmd, body=%wide.region_12.14_spmd.sunk | while | flops 2062411776 | bytes 140181296 | solution.py:204
  253.9 7.3 %multiply_reduce_fusion.7 = (f32[12,512]{1,0:T(8,128)S(1)}, f32[12,512,512]{1,2,0:T(8,128)}) fusion(f32[12,512,512]{1,2,0:T(8,128)S(1)} %fusion.154, f32[12,512]{1,0:T(8,128)S(1)} %dynamic-slice_bitcast_fusion.2, pred[512]{0:T(512)(128)(4,1)S(1)} %dynamic-slice_reduce_fusion.5, bf16[2,512,12,64]{1,3,2,0:T(8,128)(2,1)S(1)} %copy-done.5, ...), kind=kOutput, calls=%fused_computation.24.clone.1 | convolution fusion | flops 418375680 | bytes 26797568 | tf_op jit(solution)/shard_map/while/body/eval_jaxpr/qhd,khd->hqk/dot_general | solution.py:60
  261.2 7.4 %multiply_convert_fusion.4 = bf16[12,512,512]{1,2,0:T(8,128)(2,1)S(1)} fusion(f32[12,512,512]{1,2,0:T(8,128)} %get-tuple-element.388, f32[12,512,512]{1,2,0:T(8,128)S(1)} %fusion.154, f32[12,512]{1,0:T(8,128)S(1)} %get-tuple-element.389, f32[12,512]{1,0:T(8,128)S(1)} %dynamic-slice_bitcast_fusion.2, pred[512]{0:T(512)(128)(4,1)S(1)} %dynamic-slice_reduce_fusion.5), kind=kLoop, calls=%fused_computation.23.clone.1 | loop fusion | flops 18874368 | bytes 31506944 | tf_op jit(solution)/shard_map/while/body/eval_jaxpr/convert_element_type | solution.py:64
  273.0 3.8 fusion.157
  278.7 7.3 %multiply_reduce_fusion.7 = (f32[12,512]{1,0:T(8,128)S(1)}, f32[12,512,512]{1,2,0:T(8,128)}) fusion(f32[12,512,512]{1,2,0:T(8,128)S(1)} %fusion.154, f32[12,512]{1,0:T(8,128)S(1)} %dynamic-slice_bitcast_fusion.2, pred[512]{0:T(512)(128)(4,1)S(1)} %dynamic-slice_reduce_fusion.5, bf16[2,512,12,64]{1,3,2,0:T(8,128)(2,1)S(1)} %copy-done.5, ...), kind=kOutput, calls=%fused_computation.24.clone.1 | convolution fusion | flops 418375680 | bytes 26797568 | tf_op jit(solution)/shard_map/while/body/eval_jaxpr/qhd,khd->hqk/dot_general | solution.py:60
  286.0 7.4 %multiply_convert_fusion.4 = bf16[12,512,512]{1,2,0:T(8,128)(2,1)S(1)} fusion(f32[12,512,512]{1,2,0:T(8,128)} %get-tuple-element.388, f32[12,512,512]{1,2,0:T(8,128)S(1)} %fusion.154, f32[12,512]{1,0:T(8,128)S(1)} %get-tuple-element.389, f32[12,512]{1,0:T(8,128)S(1)} %dynamic-slice_bitcast_fusion.2, pred[512]{0:T(512)(128)(4,1)S(1)} %dynamic-slice_reduce_fusion.5), kind=kLoop, calls=%fused_computation.23.clone.1 | loop fusion | flops 18874368 | bytes 31506944 | tf_op jit(solution)/shard_map/while/body/eval_jaxpr/convert_element_type | solution.py:64
  297.8 3.8 fusion.157
  301.8 3.1 copy.80
  314.6 6.0 convolution_bitcast_fusion
  320.6 7.3 %pad_maximum_fusion = f32[768,3072]{0,1:T(8,128)} fusion(f32[768,768]{0,1:T(8,128)S(1)} %fusion.96, f32[768,2304]{0,1:T(8,128)} %convolution_bitcast_fusion), kind=kLoop, calls=%fused_computation.90 | loop fusion | flops 2359296 | bytes 18874368 | tf_op jit(solution)/shard_map/concatenate | solution.py:227
  328.0 2.3 convert_element_type.168
  330.3 82.7 %reduce-scatter.8.cloned.1.call-done = f32[384,768]{1,0:T(8,128)} async-done(((f32[3072,768]{1,0:T(8,128)}), f32[384,768]{1,0:T(8,128)}) %reduce-scatter.8.cloned.1.call-update) | async-done | bytes 1179664 | tf_op jit(solution)/shard_map/reduce_scatter | solution.py:184
  415.3 97.8 %reduce-scatter.4.cloned.1.call-done = f32[768,384]{0,1:T(8,128)} async-done(((f32[768,3072]{0,1:T(8,128)}), f32[768,384]{0,1:T(8,128)}) %reduce-scatter.4.cloned.1.call-update) | async-done | bytes 1179664 | tf_op jit(solution)/shard_map/reduce_scatter | solution.py:232
  519.8 38.1 %all-reduce.4 = (f32[3]{0:T(128)S(1)}, f32[]{:T(128)}) all-reduce(f32[3]{0:T(128)S(1)} %pad_maximum_fusion.2, f32[]{:T(128)S(6)} %convert_element_type.178), channel_id=1, replica_groups=mesh['dp'=4,'fsdp'=8] {'dp','fsdp'}, use_global_device_ids=true, to_apply=%region_37.38 | all-reduce | flops 4 | bytes 32 | tf_op jit(solution)/shard_map/psum | solution.py:150
  558.7 28.0 %all-reduce.5 = (bf16[3840]{0:T(1024)(128)(2,1)S(1)}, bf16[5376]{0:T(1024)(128)(2,1)S(1)}) all-reduce(f32[3840]{0:T(1024)S(1)} %constant_dynamic-update-slice_fusion.6, f32[5376]{0:T(1024)S(1)} %pad_maximum_fusion.1), channel_id=4, replica_groups=mesh['dp'=4,'fsdp'=8] {'fsdp'}, use_global_device_ids=true, to_apply=%region_22.23.clone | all-reduce | flops 9216 | bytes 55296
  586.8 9.3 %all-reduce.7 = (bf16[480]{0:T(512)(128)(2,1)S(1)}, bf16[672]{0:T(1024)(128)(2,1)S(1)}) all-reduce(bf16[480]{0:T(512)(128)(2,1)S(1)} %dynamic-slice.9, bf16[672]{0:T(1024)(128)(2,1)S(1)} %dynamic-slice.8), channel_id=1, replica_groups=mesh['dp'=4,'fsdp'=8] {'dp'}, use_global_device_ids=true, to_apply=%region_23.24 | all-reduce | flops 1152 | bytes 4608 | tf_op jit(solution)/shard_map/psum | solution.py:239
  597.3 8.3 %add_convert_fusion = bf16[1024,768]{0,1:T(8,128)(2,1)S(1)} fusion(f32[1024,768]{0,1:T(8,128)} %copy-done.19, bf16[1024,2304]{0,1:T(8,128)(2,1)} %copy-done.28, bf16[768,3072]{1,0:T(8,128)(2,1)} %all-gather.6.cloned.1.call-done), kind=kOutput, calls=%fused_computation.119 | convolution fusion | flops 3625451520 | bytes 12976128 | tf_op jit(solution)/shard_map/ne,de->nd/dot_general | solution.py:221
  610.0 2.2 convert_element_type.169
  612.1 2.2 convert_element_type.171
  614.3 4.5 reshape.154
  618.8 3.2 reduce_sum.231
  (222 shorter events, 71.6 us)
Async XLA Ops:
  7.2 44.1 %copy-start.21 = (bf16[1024,768]{1,0:T(8,128)(2,1)S(1)}, bf16[1024,768]{1,0:T(8,128)(2,1)}, u32[]{:S(2)}) copy-start(bf16[1024,768]{1,0:T(8,128)(2,1)} %param.19) | copy-start | bytes 4718596
  7.2 57.1 %all-gather.6.cloned.1.call-start = ((), (), s32[]{:S(2)}) async-start(), calls=%async_computation.3 | async-start | bytes 5308416 | tf_op jit(solution)/shard_map/all_gather | solution.py:96
  7.9 115.8 %all-gather.8.cloned.1.call-start = ((), (), s32[]{:S(2)}) async-start(), calls=%async_computation.4 | async-start | bytes 5308416 | tf_op jit(solution)/shard_map/all_gather | solution.py:100
  8.7 164.5 %all-gather.10.cloned.1.call-start = ((), (), s32[]{:S(2)}) async-start(), calls=%async_computation.5 | async-start | bytes 5308416 | tf_op jit(solution)/shard_map/all_gather | solution.py:101
  9.4 318.6 %reduce-scatter.6.cloned.1.call-start = ((), (), s32[]{:S(2)}) async-start(), calls=%async_computation.7 | async-start | bytes 10616832 | tf_op jit(solution)/shard_map/reduce_scatter | solution.py:183
  48.0 16.3 %copy-start.22 = (bf16[1024,768]{1,0:T(8,128)(2,1)S(1)}, bf16[1024,768]{1,0:T(8,128)(2,1)}, u32[]{:S(2)}) copy-start(bf16[1024,768]{1,0:T(8,128)(2,1)} %param.12) | copy-start | bytes 4718596
  97.6 2.6 copy-start.4
  107.1 2.6 copy-start.4
  113.5 4.7 copy-start
  113.5 4.7 copy-start.2
  113.5 4.7 copy-start.29
  113.5 4.7 copy-start.31
  113.5 4.7 copy-start.26
  118.2 5.1 copy-start.24
  123.3 49.8 %copy-start.12 = (f32[1024,768]{0,1:T(8,128)}, f32[1024,768]{0,1:T(8,128)S(1)}, u32[]{:S(2)}) copy-start(f32[1024,768]{0,1:T(8,128)S(1)} %get-tuple-element.244) | copy-start | bytes 9437188
  123.8 49.4 %copy-start.44 = (f32[1,4,2,128]{3,1,2,0:T(4,128)S(1)}, f32[1,4,2,128]{3,1,2,0:T(4,128)}, u32[]{:S(2)}) copy-start(f32[1,4,2,128]{3,1,2,0:T(4,128)} %copy.98) | copy-start | bytes 12292
  123.8 49.4 %copy-start.45 = (f32[768]{0:T(1024)S(1)}, f32[768]{0:T(1024)}, u32[]{:S(2)}) copy-start(f32[768]{0:T(1024)} %get-tuple-element.256) | copy-start | bytes 9220
  173.2 18.9 %copy-start.48 = (f32[1024,3072]{1,0:T(8,128)S(1)}, f32[1024,3072]{1,0:T(8,128)}, u32[]{:S(2)}) copy-start(f32[1024,3072]{1,0:T(8,128)} %get-tuple-element.268) | copy-start | bytes 37748740
  185.8 2.9 copy-start.37
  185.8 2.9 copy-start.38
  186.8 5.2 slice-start
  188.8 3.3 slice-start.1
  192.0 12.3 %copy-start.27 = (bf16[1024,768]{0,1:T(8,128)(2,1)}, bf16[1024,768]{0,1:T(8,128)(2,1)S(1)}, u32[]{:S(2)}) copy-start(bf16[1024,768]{0,1:T(8,128)(2,1)S(1)} %get-tuple-element.238) | copy-start | bytes 4718596
  192.1 14.9 %copy-start.13 = (f32[1024,768]{0,1:T(8,128)S(1)}, f32[1024,768]{0,1:T(8,128)}, u32[]{:S(2)}) copy-start(f32[1024,768]{0,1:T(8,128)} %copy-done.12) | copy-start | bytes 9437188
  204.3 2.6 copy-start.47
  214.7 198.2 %reduce-scatter.8.cloned.1.call-start = ((), (), s32[]{:S(2)}) async-start(), calls=%async_computation.8 | async-start | bytes 10616832 | tf_op jit(solution)/shard_map/reduce_scatter | solution.py:184
  225.2 287.9 %reduce-scatter.4.cloned.1.call-start = ((), (), s32[]{:S(2)}) async-start(), calls=%async_computation.6 | async-start | bytes 10616832 | tf_op jit(solution)/shard_map/reduce_scatter | solution.py:232
  225.8 12.2 %copy-start.14 = (f32[1024,768]{0,1:T(8,128)S(1)}, f32[1024,768]{0,1:T(8,128)}, u32[]{:S(2)}) copy-start(f32[1024,768]{0,1:T(8,128)} %copy-done.12) | copy-start | bytes 9437188
  247.7 4.0 copy-start.1
  247.7 4.0 copy-start.3
  247.7 4.0 copy-start.30
  247.7 4.0 copy-start.32
  261.2 7.4 %copy-start.15 = (bf16[2,512,12,64]{1,3,2,0:T(8,128)(2,1)S(1)}, bf16[2,512,12,64]{1,3,2,0:T(8,128)(2,1)}, u32[]{:S(2)}) copy-start(bf16[2,512,12,64]{1,3,2,0:T(8,128)(2,1)} %get-tuple-element.427) | copy-start | bytes 4718596 | tf_op jit(solution)/shard_map/while
  286.0 7.4 %copy-start.15 = (bf16[2,512,12,64]{1,3,2,0:T(8,128)(2,1)S(1)}, bf16[2,512,12,64]{1,3,2,0:T(8,128)(2,1)}, u32[]{:S(2)}) copy-start(bf16[2,512,12,64]{1,3,2,0:T(8,128)(2,1)} %get-tuple-element.427) | copy-start | bytes 4718596 | tf_op jit(solution)/shard_map/while
  301.8 3.6 copy-start.17
  309.7 2.3 copy-start.25
  312.0 2.6 copy-start.23
  327.9 187.3 %copy-start.46 = (s32[2]{0:T(128)S(1)}, s32[2]{0:T(128)}, u32[]{:S(2)}) copy-start(s32[2]{0:T(128)} %param.18) | copy-start | bytes 28
  327.9 229.9 %copy-start.9 = (bf16[2,512,12,64]{1,3,2,0:T(8,128)(2,1)S(1)}, bf16[2,512,12,64]{1,3,2,0:T(8,128)(2,1)}, u32[]{:S(2)}) copy-start(bf16[2,512,12,64]{1,3,2,0:T(8,128)(2,1)} %get-tuple-element.102) | copy-start | bytes 4718596
  327.9 282.0 %all-reduce.11.cloned.1.call-start = ((), (), s32[]{:S(2)}) async-start(), calls=%async_computation.10 | async-start | bytes 2359296 | tf_op jit(solution)/shard_map/psum | solution.py:240
  415.1 143.4 %copy-start.36 = (f32[768]{0:T(1024)S(1)}, f32[768]{0:T(1024)}, u32[]{:S(2)}) copy-start(f32[768]{0:T(1024)} %get-tuple-element.239) | copy-start | bytes 9220
  415.1 143.4 %copy-start.43 = (f32[768]{0:T(1024)S(1)}, f32[768]{0:T(1024)}, u32[]{:S(2)}) copy-start(f32[768]{0:T(1024)} %get-tuple-element.180) | copy-start | bytes 9220
  415.1 143.4 %copy-start.42 = (f32[768]{0:T(1024)S(1)}, f32[768]{0:T(1024)}, u32[]{:S(2)}) copy-start(f32[768]{0:T(1024)} %get-tuple-element.185) | copy-start | bytes 9220
  415.1 143.5 %copy-start.34 = (f32[768]{0:T(1024)S(1)}, f32[768]{0:T(1024)}, u32[]{:S(2)}) copy-start(f32[768]{0:T(1024)} %get-tuple-element.237) | copy-start | bytes 9220
  415.2 143.5 %copy-start.39 = (f32[768]{0:T(1024)S(1)}, f32[768]{0:T(1024)}, u32[]{:S(2)}) copy-start(f32[768]{0:T(1024)} %get-tuple-element.182) | copy-start | bytes 9220
  415.2 143.5 %copy-start.40 = (f32[768]{0:T(1024)S(1)}, f32[768]{0:T(1024)}, u32[]{:S(2)}) copy-start(f32[768]{0:T(1024)} %get-tuple-element.187) | copy-start | bytes 9220
  415.2 143.5 %copy-start.41 = (f32[3072]{0:T(1024)S(1)}, f32[3072]{0:T(1024)}, u32[]{:S(2)}) copy-start(f32[3072]{0:T(1024)} %get-tuple-element.270) | copy-start | bytes 36868
  415.2 199.1 %all-gather.12.cloned.1.call-start = ((), (), s32[]{:S(2)}) async-start(), calls=%async_computation.9 | async-start | bytes 2949120 | tf_op jit(solution)/shard_map/all_gather | solution.py:236
  (18 other events, 29.5 us)
Sparse Core Ops, SparseCore 0:
  9.6 54.6 all-gather.5
  65.9 50.1 all-gather.7
  117.7 49.8 all-gather.9
  214.9 97.9 reduce-scatter.5
  315.1 97.8 reduce-scatter.7
  415.2 97.8 reduce-scatter.3
  516.8 53.6 all-reduce.10
  572.9 37.4 all-gather.11
